TPU v7x, 32 devices: a whole 2x2x4 slice. The times are simulated.
32 devices in a mesh: section: 2 (over x), row: 4 (over y, core), col: 4 (over z).
Axes of the slice: x: 2, y: 2, z: 4, core: 2. Of those that a mesh axis runs over, the one named last changes fastest.
Arguments:
- stash_inputs: bfloat16 [2, 4, 512, 12288], P('section', None, 'row', 'col'), may hold values from -16 to 16
- stash_hidden: bfloat16 [2, 4, 512, 24576], P('section', None, 'col', 'row'), may hold values from -6 to 6
- grad_in: bfloat16 [2, 512, 12288], P('section', 'row', 'col'), may hold values from -6 to 6
- w_in: bfloat16 [2, 12288, 24576], P('section', 'col', 'row'), may hold values from -0.0546875 to 0.0546875
- b_in: float32 [2, 24576], P('section', 'row'), may hold values from -3 to 3
- w_out: bfloat16 [2, 24576, 12288], P('section', 'row', 'col'), may hold values from -0.0390625 to 0.0390625
- b_out: float32 [2, 12288], P('section', 'col'), may hold values from -3 to 3
- ln_gain: float32 [2, 12288], P('section', 'col'), may hold values from 0.4 to 1.6
- plan: int32 [2, 2], P('section'), may hold values from 0 to 3, as said below
Outputs:
- act_recv: bfloat16 [2, 512, 12288], P('section', 'row', 'col')
- grad_recv: bfloat16 [2, 512, 12288], P('section', 'row', 'col')
- saved_hidden: bfloat16 [2, 512, 24576], P('section', 'col', 'row')
Inputs may be any that keep to these rules, and one draw needn't show every extreme that they name: plan[s, 0] is the stash slot of the micro-batch that section s takes backward, plan[s, 1] that of the one it takes forward; the two differ.
All inputs are finite; a program needn't handle non-finite values.
Results may differ from a plain program's by a relative error of at most 0.015.
Values may be sent and summed in bfloat16 or wider, within the bound.
A program may use at most 192 MiB of HBM per device.

v0:
```python
import functools

import jax
import jax.numpy as jnp
from jax import lax
from jax.experimental import pallas as pl
from jax.experimental.pallas import tpu as pltpu
from jax.sharding import PartitionSpec as P

MESH = pl.DeviceIdType.MESH
F32 = jnp.float32
BF16 = jnp.bfloat16
LANE = 128
EPSILON = 1e-05
ROOT = 0.7978845608028654
CUBIC = 0.044715
WIDTH = 512
STRIP = 256


def gelu_value(values):
    inner = ROOT * (values + CUBIC * values * values * values)
    return 0.5 * values * (1.0 + jnp.tanh(inner))


def gelu_slope(values):
    inner = ROOT * (values + CUBIC * values * values * values)
    tangent = jnp.tanh(inner)
    return 0.5 * (1.0 + tangent) + 0.5 * values * (1.0 - tangent * tangent) * ROOT * (
        1.0 + 3.0 * CUBIC * values * values
    )


def flipped(index, bit):
    return index + bit * (1 - 2 * ((index // bit) % 2))


def flipped_by(index, mask):
    bit = 1
    while bit <= mask:
        if mask & bit:
            index = flipped(index, bit)
        bit *= 2
    return index


def strips(columns, strip, body):
    @pl.loop(0, columns // strip)
    def _(step):
        body(pl.ds(pl.multiple_of(step * strip, strip), strip))


def kernel(
    n, ranks, sections, width, pieces,
    fwd_in, bwd_in, bwd_hidden, upstream, b_in, b_out, gain, w_in, w_out,
    act_recv, grad_recv, saved,
    up_all, normed_all, acc, first_in, first_out, second_in, second_out,
    part, moved, held, total, own, stats, stat_sent, stat_got,
    half_sent, half_got, side_sent, side_got, final,
    first_sem, second_sem, sum_send, sum_recv, spread_send, spread_recv,
    gather_send, gather_recv, stat_send, stat_recv,
    half_send, half_recv, side_send, side_recv, final_send, final_recv,
    credit, half_free, side_free,
):
    col = lax.axis_index("col")
    row = lax.axis_index("row")
    section = lax.axis_index("section")
    tokens, features = up_all.shape
    hidden_units = w_in.shape[1]
    own_rows = tokens // ranks
    block = tokens // n
    chunks = hidden_units // width
    queue = 2 * chunks
    piece = features // pieces
    side = ranks // 2
    last = n - 1
    inverse = 1.0 / (features * n)
    strip = min(STRIP, features)

    barrier = pltpu.get_barrier_semaphore()
    for away in range(1, n):
        pl.semaphore_signal(barrier, 1, device_id={"col": (col + away) % n}, device_id_type=MESH)
    pl.semaphore_signal(barrier, 1, device_id={"row": flipped(row, 1)}, device_id_type=MESH)
    pl.semaphore_signal(barrier, 1, device_id={"row": flipped(row, side)}, device_id_type=MESH)
    for away in (1, sections - 1):
        pl.semaphore_signal(
            barrier, 1, device_id={"section": (section + away) % sections}, device_id_type=MESH
        )
    pl.semaphore_wait(barrier, n - 1 + 2 + 2)

    def rows_of(index):
        return pl.ds(pl.multiple_of(index * own_rows, own_rows), own_rows)

    def block_of(index):
        return pl.ds(pl.multiple_of(index * block, block), block)

    def gather_copy(which, source, target, index, hop):
        bit = side if hop == 0 else 1
        place = rows_of(index)
        return pltpu.make_async_remote_copy(
            src_ref=source if source is not None else target.at[place],
            dst_ref=target.at[place],
            send_sem=gather_send.at[which, hop],
            recv_sem=gather_recv.at[which, hop],
            device_id={"row": flipped(row, bit)},
            device_id_type=MESH,
        )

    gather_copy(0, upstream, up_all, row, 0).start()
    gather_copy(0, upstream, up_all, row, 1).start()

    def take_up(cols):
        up_all[rows_of(row), cols] = upstream[:, cols]
        acc[:, cols] = jnp.zeros((tokens, cols.size), F32)

    def first_copy(index, start):
        slot = lax.rem(index, 2)

        @pl.when(index < chunks)
        def _():
            place = pl.ds(pl.multiple_of(index * width, width), width)
            copy = pltpu.make_async_copy(w_out.at[place], first_out.at[slot], first_sem.at[slot])
            copy.start() if start else copy.wait()

        @pl.when(index >= chunks)
        def _():
            place = pl.ds(pl.multiple_of((index - chunks) * width, width), width)
            copy = pltpu.make_async_copy(w_in.at[:, place], first_in.at[slot], first_sem.at[slot])
            copy.start() if start else copy.wait()

    def second_copy(index, start):
        slot = lax.rem(index, 2)

        @pl.when(index < chunks)
        def _():
            place = pl.ds(pl.multiple_of(index * width, width), width)
            copy = pltpu.make_async_copy(w_in.at[:, place], second_in.at[slot], second_sem.at[slot])
            copy.start() if start else copy.wait()

        @pl.when(index >= chunks)
        def _():
            place = pl.ds(pl.multiple_of((index - chunks) * width, width), width)
            copy = pltpu.make_async_copy(w_out.at[place], second_out.at[slot], second_sem.at[slot])
            copy.start() if start else copy.wait()

    first_copy(jnp.int32(0), True)
    second_copy(jnp.int32(0), True)
    strips(features, strip, take_up)

    lane = lax.broadcasted_iota(jnp.int32, (own_rows, LANE), 1)

    def packed(columns):
        values = jnp.zeros((own_rows, LANE), F32)
        for place, column in enumerate(columns):
            values = jnp.where(lane == place, column, values)
        return values

    def stat_copy(which, away):
        return pltpu.make_async_remote_copy(
            src_ref=stat_sent.at[which],
            dst_ref=stat_got.at[which, away - 1],
            send_sem=stat_send.at[which, away - 1],
            recv_sem=stat_recv.at[which, away - 1],
            device_id={"col": (col + away) % n},
            device_id_type=MESH,
        )

    def summed(which):
        values = stat_sent[which]
        for away in range(1, n):
            stat_copy(which, away).wait_recv()
            values = values + stat_got[which, away - 1]
        return values

    def reduced(source):
        def one(step, sums):
            cols = pl.ds(pl.multiple_of(step * strip, strip), strip)
            values = source(cols)
            return tuple(
                s + jnp.sum(v, axis=1, keepdims=True) for s, v in zip(sums, values, strict=True)
            )

        zero = jnp.zeros((own_rows, 1), F32)
        return lax.fori_loop(0, features // strip, one, (zero,) * 2)

    def moments(ref):
        def source(cols):
            values = ref[:, cols].astype(F32)
            return values, values * values

        return reduced(source)

    stat_sent[0] = packed(moments(fwd_in) + moments(bwd_in))
    for away in range(1, n):
        stat_copy(0, away).start()
    sums = summed(0)

    def scale_of(total_sum, squares):
        mean = total_sum * inverse
        return mean, lax.rsqrt(squares * inverse - mean * mean + EPSILON)

    stats[...] = packed(
        scale_of(sums[:, 0:1], sums[:, 1:2]) + scale_of(sums[:, 2:3], sums[:, 3:4])
    )

    def normalize(cols):
        hat = (fwd_in[:, cols].astype(F32) - stats[:, 0:1]) * stats[:, 1:2]
        normed_all[rows_of(row), cols] = (hat * gain[:, cols]).astype(BF16)

    strips(features, strip, normalize)
    gather_copy(1, None, normed_all, row, 0).start()
    gather_copy(1, None, normed_all, row, 1).start()

    def pass_on(which, target):
        far = flipped(row, side)
        gather_copy(which, None, target, far, 0).wait_recv()
        gather_copy(which, None, target, far, 2).start()

    def gathered(which, target):
        near = flipped(row, 1)
        gather_copy(which, None, target, near, 1).wait_recv()
        gather_copy(which, None, target, flipped(near, side), 2).wait_recv()
        for hop in range(3):
            gather_copy(which, None, target, row, hop).wait_send()

    pass_on(0, up_all)
    gathered(0, up_all)

    def neighbour(way):
        return jnp.minimum(col + 1, last) if way == 0 else jnp.maximum(col - 1, 0)

    def place_in_line(way):
        return col if way == 0 else last - col

    def sum_copy(way, index, hop, target):
        return pltpu.make_async_remote_copy(
            src_ref=part.at[lax.rem(index, n), block_of(target)],
            dst_ref=moved.at[way, lax.rem(index, 3), hop],
            send_sem=sum_send.at[way, lax.rem(index + hop, 2), hop],
            recv_sem=sum_recv.at[way, lax.rem(index, 3), hop],
            device_id={"col": neighbour(way)},
            device_id_type=MESH,
        )

    def spread_copy(way, index, hop, origin):
        slot = lax.rem(index, n + 1)
        return pltpu.make_async_remote_copy(
            src_ref=held.at[slot, block_of(origin)],
            dst_ref=held.at[slot, block_of(origin)],
            send_sem=spread_send.at[way, lax.rem(index + hop, 2), hop],
            recv_sem=spread_recv.at[way, lax.rem(index, 3), hop],
            device_id={"col": neighbour(way)},
            device_id_type=MESH,
        )

    def valid(index):
        return jnp.logical_and(index >= 0, index < queue)

    def sum_target(way, hop):
        at = last - hop + place_in_line(way)
        return at if way == 0 else last - at

    def spread_origin(way, hop):
        return col - hop if way == 0 else col + hop

    def sum_step(index, hop):
        for way in range(2):
            at = place_in_line(way)

            @pl.when(valid(index) & (at <= hop) & (at < last))
            def _():
                target = sum_target(way, hop)
                if hop > 0:

                    @pl.when(at > 0)
                    def _():
                        sum_copy(way, index, hop - 1, target).wait_recv()
                        slot = lax.rem(index, n)
                        mine = part[slot, block_of(target)].astype(F32)
                        more = moved[way, lax.rem(index, 3), hop - 1].astype(F32)
                        part[slot, block_of(target)] = (mine + more).astype(BF16)

                sum_copy(way, index, hop, target).start()

    def sum_sent(index, hop):
        for way in range(2):
            at = place_in_line(way)

            @pl.when(valid(index) & (at <= hop) & (at < last))
            def _():
                sum_copy(way, index, hop, sum_target(way, hop)).wait_send()

    def spread_step(index, hop):
        for way in range(2):
            at = place_in_line(way)

            @pl.when(valid(index) & (at >= hop))
            def _():
                origin = spread_origin(way, hop)
                if hop > 0:
                    spread_copy(way, index, hop - 1, origin).wait_recv()

                @pl.when(at < last)
                def _():
                    spread_copy(way, index, hop, origin).start()

    def spread_sent(index, hop):
        for way in range(2):
            at = place_in_line(way)

            @pl.when(valid(index) & (at >= hop) & (at < last))
            def _():
                spread_copy(way, index, hop, spread_origin(way, hop)).wait_send()

    def spread_done(index):
        for way in range(2):

            @pl.when(place_in_line(way) == last)
            def _():
                spread_copy(way, index, n - 2, spread_origin(way, last)).wait_recv()

    def activate(index):
        slot = lax.rem(index, n)
        out_slot = lax.rem(index, n + 1)
        for way in range(2):

            @pl.when(place_in_line(way) > 0)
            def _():
                sum_copy(way, index, n - 2, col).wait_recv()

        total[...] = part[slot, block_of(col)].astype(F32)
        for way in range(2):

            @pl.when(place_in_line(way) > 0)
            def _():
                total[...] += moved[way, lax.rem(index, 3), n - 2].astype(F32)

        tile = min(STRIP, width)

        @pl.when(index < chunks)
        def _():
            for at in range(0, width, tile):
                cols = pl.ds(pl.multiple_of(index * width + at, tile), tile)
                slope = gelu_slope(bwd_hidden[:, cols].astype(F32))
                held[out_slot, block_of(col), at : at + tile] = (
                    total[:, at : at + tile] * slope
                ).astype(BF16)

        @pl.when(index >= chunks)
        def _():
            for at in range(0, width, tile):
                cols = pl.ds(pl.multiple_of((index - chunks) * width + at, tile), tile)
                values = total[:, at : at + tile] + b_in[:, cols]
                saved[:, cols] = values.astype(BF16)
                held[out_slot, block_of(col), at : at + tile] = gelu_value(values).astype(BF16)

    both_last = (((1,), (1,)), ((), ()))
    both_inner = (((1,), (0,)), ((), ()))

    def first_product(index):
        slot = lax.rem(index, 2)
        out_slot = lax.rem(index, n)
        tile = min(256, width)

        @pl.when(index < chunks)
        def _():
            for at in range(0, width, tile):
                part[out_slot, :, at : at + tile] = lax.dot_general(
                    up_all[...], first_out[slot, at : at + tile, :], both_last,
                    preferred_element_type=F32,
                ).astype(BF16)

        @pl.when(index >= chunks)
        def _():
            for at in range(0, width, tile):
                part[out_slot, :, at : at + tile] = lax.dot_general(
                    normed_all[...], first_in[slot, :, at : at + tile], both_inner,
                    preferred_element_type=F32,
                ).astype(BF16)

    def second_product(index):
        slot = lax.rem(index, 2)
        in_slot = lax.rem(index, n + 1)
        tile = min(256, features)
        group = 2 if features % (2 * tile) == 0 else 1

        @pl.when(index < chunks)
        def _():
            @pl.loop(0, features // (tile * group))
            def _(step):
                for k in range(group):
                    at = pl.ds(pl.multiple_of((step * group + k) * tile, tile), tile)
                    acc[:, at] += lax.dot_general(
                        held[in_slot], second_in[slot, at, :], both_last,
                        preferred_element_type=F32,
                    )

        @pl.when(index >= chunks)
        def _():
            @pl.loop(0, features // (tile * group))
            def _(step):
                for k in range(group):
                    at = pl.ds(pl.multiple_of((step * group + k) * tile, tile), tile)
                    acc[:, at] += lax.dot_general(
                        held[in_slot], second_out[slot, :, at], both_inner,
                        preferred_element_type=F32,
                    )

    def half_copy(which, k):
        return pltpu.make_async_remote_copy(
            src_ref=half_sent.at[k],
            dst_ref=half_got.at[k],
            send_sem=half_send.at[which, k],
            recv_sem=half_recv.at[which, k],
            device_id={"row": flipped(row, 1)},
            device_id_type=MESH,
        )

    def side_copy(which, p):
        return pltpu.make_async_remote_copy(
            src_ref=side_sent.at[p],
            dst_ref=side_got.at[p],
            send_sem=side_send.at[which, p],
            recv_sem=side_recv.at[which, p],
            device_id={"row": flipped(row, side)},
            device_id_type=MESH,
        )

    def final_copy(which, p):
        target = grad_recv if which == 0 else act_recv
        away = sections - 1 if which == 0 else 1
        cols = pl.ds(p * piece, piece)
        return pltpu.make_async_remote_copy(
            src_ref=final.at[which, :, cols],
            dst_ref=target.at[:, cols],
            send_sem=final_send.at[which, p],
            recv_sem=final_recv.at[which, p],
            device_id={"section": (section + away) % sections},
            device_id_type=MESH,
        )

    def fold_near(which):
        if which == 1:
            pl.semaphore_wait(half_free, 1)
        for k in (1, 0):
            index = flipped_by(row, 1 + side * k)

            def cut(cols):
                half_sent[k, :, cols] = acc[rows_of(index), cols].astype(BF16)

            strips(features, strip, cut)
            half_copy(which, k).start()

    def fold_far(which):
        half_copy(which, 1).wait_recv()
        if which == 1:
            pl.semaphore_wait(side_free, 1)
        far = flipped(row, side)
        for p in range(pieces):
            cols = pl.ds(p * piece, piece)
            side_sent[p] = (
                acc[rows_of(far), cols] + half_got[1, :, cols].astype(F32)
            ).astype(BF16)
            side_copy(which, p).start()
        half_copy(which, 0).wait_recv()

        def keep(cols):
            own[:, cols] = acc[rows_of(row), cols] + half_got[0, :, cols].astype(F32)

        strips(features, strip, keep)
        for k in range(2):
            half_copy(which, k).wait_send()
        if which == 0:
            pl.semaphore_signal(
                half_free, 1, device_id={"row": flipped(row, 1)}, device_id_type=MESH
            )

            def clear(cols):
                acc[:, cols] = jnp.zeros((tokens, cols.size), F32)

            strips(features, strip, clear)

    def backward_hat(cols):
        return (bwd_in[:, cols].astype(F32) - stats[:, 2:3]) * stats[:, 3:4]

    def backward_sums():
        for p in range(pieces):
            side_copy(0, p).wait_recv()
            cols = pl.ds(p * piece, piece)
            own[:, cols] = (own[:, cols] + side_got[p].astype(F32)) * gain[:, cols]
        for p in range(pieces):
            side_copy(0, p).wait_send()
        pl.semaphore_signal(
            side_free, 1, device_id={"row": flipped(row, side)}, device_id_type=MESH
        )

        def source(cols):
            scaled = own[:, cols]
            return scaled, scaled * backward_hat(cols)

        stat_sent[1] = packed(reduced(source))
        for away in range(1, n):
            stat_copy(1, away).start()

    def backward_end():
        sums = summed(1) * inverse
        stats[...] = packed((stats[:, 0:1], stats[:, 1:2], stats[:, 2:3], stats[:, 3:4], sums[:, 0:1], sums[:, 1:2]))

        def finish(cols):
            values = own[:, cols] - stats[:, 4:5] - backward_hat(cols) * stats[:, 5:6]
            final[0, :, cols] = (
                upstream[:, cols].astype(F32) + stats[:, 3:4] * values
            ).astype(BF16)

        strips(features, strip, finish)
        for p in range(pieces):
            final_copy(0, p).start()

    turn = 2 * n - 2
    steps = queue + turn
    middle = chunks - 1 + turn

    def step(m, carry):
        first_ready = valid(m)
        second = m - turn

        for way in range(2):

            @pl.when((m >= 2) & (place_in_line(way) < last))
            def _():
                pl.semaphore_wait(credit.at[way], 1)

        @pl.when(m + 1 < queue)
        def _():
            first_copy(m + 1, True)

        @pl.when((second + 1 >= 1) & (second + 1 < queue))
        def _():
            second_copy(second + 1, True)

        for hop in range(1, n - 1):
            sum_step(m - hop, hop)

        @pl.when(valid(m - last))
        def _():
            activate(m - last)

        for hop in range(n - 1):
            spread_step(m - last - hop, hop)

        @pl.when(m == min(4, chunks - 1))
        def _():
            pass_on(1, normed_all)

        @pl.when(m == chunks)
        def _():
            gathered(1, normed_all)

        @pl.when(first_ready)
        def _():
            first_copy(m, False)
            first_product(m)

        sum_step(m, 0)

        @pl.when(m == middle + 1)
        def _():
            fold_far(0)

        @pl.when(m == middle + 3)
        def _():
            backward_sums()

        @pl.when(m == middle + 4)
        def _():
            backward_end()

        @pl.when(valid(second))
        def _():
            spread_done(second)
            second_copy(second, False)
            second_product(second)

        @pl.when(m == middle)
        def _():
            fold_near(0)

        for hop in range(n - 1):
            sum_sent(m - 1 - hop, hop)
            spread_sent(m - 1 - last - hop, hop)

        for way in range(2):

            @pl.when((m < steps - 2) & (place_in_line(way) > 0))
            def _():
                pl.semaphore_signal(
                    credit.at[way], 1, device_id={"col": neighbour(1 - way)}, device_id_type=MESH
                )

        return carry

    lax.fori_loop(0, steps, step, 0)

    fold_near(1)
    fold_far(1)
    for p in range(pieces):
        cols = pl.ds(p * piece, piece)
        side_copy(1, p).wait_recv()
        final[1, :, cols] = (
            own[:, cols] + side_got[p].astype(F32) + b_out[:, cols] + fwd_in[:, cols].astype(F32)
        ).astype(BF16)
        final_copy(1, p).start()
    for p in range(pieces):
        side_copy(1, p).wait_send()
    for which in range(2):
        for away in range(1, n):
            stat_copy(which, away).wait_send()
        for p in range(pieces):
            final_copy(which, p).wait()


def cut_count(features):
    return max(p for p in range(1, 5) if features % (p * LANE) == 0)


def whole_layer(shape, *operands):
    n, ranks, sections = shape["col"], shape["row"], shape["section"]
    fwd_in, w_in = operands[0], operands[7]
    own_rows, features = fwd_in.shape
    hidden_units = w_in.shape[1]
    tokens = own_rows * ranks
    block = tokens // n
    width = WIDTH if n <= 8 else WIDTH // 2
    pieces = cut_count(features)
    dma = pltpu.SemaphoreType.DMA
    in_vmem = pl.BlockSpec(memory_space=pltpu.VMEM)
    anywhere = pl.BlockSpec(memory_space=pl.ANY)
    scratch = [
        pltpu.VMEM((tokens, features), BF16),
        pltpu.VMEM((tokens, features), BF16),
        pltpu.VMEM((tokens, features), F32),
        pltpu.VMEM((2, features, width), BF16),
        pltpu.VMEM((2, width, features), BF16),
        pltpu.VMEM((2, features, width), BF16),
        pltpu.VMEM((2, width, features), BF16),
        pltpu.VMEM((n, tokens, width), BF16),
        pltpu.VMEM((2, 3, n - 1, block, width), BF16),
        pltpu.VMEM((n + 1, tokens, width), BF16),
        pltpu.VMEM((block, width), F32),
        pltpu.VMEM((own_rows, features), F32),
        pltpu.VMEM((own_rows, LANE), F32),
        pltpu.VMEM((2, own_rows, LANE), F32),
        pltpu.VMEM((2, n - 1, own_rows, LANE), F32),
        pltpu.VMEM((2, own_rows, features), BF16),
        pltpu.VMEM((2, own_rows, features), BF16),
        pltpu.VMEM((pieces, own_rows, features // pieces), BF16),
        pltpu.VMEM((pieces, own_rows, features // pieces), BF16),
        pltpu.VMEM((2, own_rows, features), BF16),
        dma((2,)),
        dma((2,)),
        dma((2, 2, n - 1)),
        dma((2, 3, n - 1)),
        dma((2, 2, n - 1)),
        dma((2, 3, n - 1)),
        dma((2, 3)),
        dma((2, 3)),
        dma((2, n - 1)),
        dma((2, n - 1)),
        dma((2, 2)),
        dma((2, 2)),
        dma((2, pieces)),
        dma((2, pieces)),
        dma((2, pieces)),
        dma((2, pieces)),
        pltpu.SemaphoreType.REGULAR((2,)),
        pltpu.SemaphoreType.REGULAR,
        pltpu.SemaphoreType.REGULAR,
    ]
    return pl.pallas_call(
        functools.partial(kernel, n, ranks, sections, width, pieces),
        out_shape=(
            jax.ShapeDtypeStruct((own_rows, features), BF16),
            jax.ShapeDtypeStruct((own_rows, features), BF16),
            jax.ShapeDtypeStruct((block, hidden_units), BF16),
        ),
        in_specs=[in_vmem] * 7 + [anywhere] * 2,
        out_specs=(anywhere, anywhere, in_vmem),
        scratch_shapes=scratch,
        name="layer",
        cost_estimate=pl.CostEstimate(
            flops=8 * tokens * features * hidden_units,
            bytes_accessed=8 * features * hidden_units,
            transcendentals=0,
        ),
        compiler_params=pltpu.CompilerParams(
            collective_id=0, has_side_effects=True, vmem_limit_bytes=67043328
        ),
    )(*operands)


def body(shape, stash_inputs, stash_hidden, grad_in, w_in, b_in, w_out, b_out, ln_gain, plan):
    def picked(stash, slot):
        return lax.dynamic_index_in_dim(stash[0], slot, 0, keepdims=False)

    bwd_slot = plan[0, 0]
    fwd_slot = plan[0, 1]
    act, grad, saved = whole_layer(
        shape,
        picked(stash_inputs, fwd_slot),
        picked(stash_inputs, bwd_slot),
        picked(stash_hidden, bwd_slot),
        grad_in[0],
        b_in,
        b_out,
        ln_gain,
        w_in[0],
        w_out[0],
    )
    return (act[None], grad[None], saved[None])


def solution(mesh):
    in_specs = (
        P("section", None, "row", "col"),
        P("section", None, "col", "row"),
        P("section", "row", "col"),
        P("section", "col", "row"),
        P("section", "row"),
        P("section", "row", "col"),
        P("section", "col"),
        P("section", "col"),
        P("section", None),
    )
    out_specs = (P("section", "row", "col"), P("section", "row", "col"), P("section", "col", "row"))
    return jax.shard_map(
        functools.partial(body, dict(mesh.shape)),
        mesh=mesh,
        in_specs=in_specs,
        out_specs=out_specs,
        check_vma=False,
    )
```

profile of v0, /device:TPU:0, one launch (start us, length us, event | category | flops | bytes accessed | tf_op | source)
XLA Modules:
  0.0 380.5 jit_solution(16407369695755725731)
XLA Ops:
  0.6 1.3 fusion
  5.8 2.6 dynamic-slice_bitcast_fusion.1
  8.4 2.7 dynamic-slice_bitcast_fusion.bwd_hidden
  11.1 363.9 %layer.1 = (bf16[128,3072]{1,0:T(8,128)(2,1)}, bf16[128,3072]{1,0:T(8,128)(2,1)}, bf16[128,6144]{1,0:T(8,128)(2,1)}) custom-call(bf16[128,3072]{1,0:T(8,128)(2,1)} %get-tuple-element.10.fwd_in, bf16[128,3072]{1,0:T(8,128)(2,1)} %get-tuple-element.9.bwd_in, bf16[128,6144]{1,0:T(8,128)(2,1)} %dynamic-slice_bitcast_fusion.bwd_hidden, ...), custom_call_target="tpu_custom_call" | custom-call | flops 77309411328 | bytes 150994944 | tf_op jit(solution)/shard_map/layer/pallas_call | solution.py:679
  375.1 0.0 copy-start
  375.1 2.2 copy.15
  377.2 2.1 copy.16
  379.3 0.0 copy-done
  379.3 1.1 copy.17
Async XLA Ops:
  375.1 4.3 %copy-start = (bf16[128,6144]{1,0:T(8,128)(2,1)S(1)}, bf16[128,6144]{1,0:T(8,128)(2,1)}, u32[]{:S(2)}) copy-start(bf16[128,6144]{1,0:T(8,128)(2,1)} %get-tuple-element.8) | copy-start | bytes 4718596
where the time goes:
time: 381 us; the launch traced here: 380 us
  Pallas kernels  364 us (96%)
  local copies, waits for them, and re-layouts  12 us (3%)
  between operations  4.53 us (1%)
    pallas_call x1, Pallas kernels, whole_layer(): pl.pallas_call(functools.partial(kernel, n, ranks, sections, width, piece...  364 us

commit v1 on v0

--- a/solution.py
+++ b/solution.py
@@ -14,7 +14,7 @@
 EPSILON = 1e-05
 ROOT = 0.7978845608028654
 CUBIC = 0.044715
-WIDTH = 512
+WIDTH = 384
 STRIP = 256
 
 
@@ -52,12 +52,12 @@
 
 def kernel(
     n, ranks, sections, width, pieces,
-    fwd_in, bwd_in, bwd_hidden, upstream, b_in, b_out, gain, w_in, w_out,
+    plan, b_in, b_out, gain, stash_inputs, stash_hidden, upstream, w_in, w_out,
     act_recv, grad_recv, saved,
     up_all, normed_all, acc, first_in, first_out, second_in, second_out,
     part, moved, held, total, own, stats, stat_sent, stat_got,
-    half_sent, half_got, side_sent, side_got, final,
-    first_sem, second_sem, sum_send, sum_recv, spread_send, spread_recv,
+    half_sent, half_got, side_sent, side_got, final, kept, slopes,
+    start_sem, slope_sem, first_sem, second_sem, sum_send, sum_recv, spread_send, spread_recv,
     gather_send, gather_recv, stat_send, stat_recv,
     half_send, half_recv, side_send, side_recv, final_send, final_recv,
     credit, half_free, side_free,
@@ -71,6 +71,8 @@
     block = tokens // n
     chunks = hidden_units // width
     queue = 2 * chunks
+    bwd_slot = plan[0, 0]
+    fwd_slot = plan[0, 1]
     piece = features // pieces
     side = ranks // 2
     last = n - 1
@@ -88,17 +90,29 @@
         )
     pl.semaphore_wait(barrier, n - 1 + 2 + 2)
 
+    def chunk_of(unit):
+        return lax.rem(unit, chunks)
+
+    def backward(unit):
+        return unit < chunks
+
+    def fwd_in(cols):
+        return kept[fwd_slot, :, cols].astype(F32)
+
+    def bwd_in(cols):
+        return kept[bwd_slot, :, cols].astype(F32)
+
     def rows_of(index):
         return pl.ds(pl.multiple_of(index * own_rows, own_rows), own_rows)
 
     def block_of(index):
         return pl.ds(pl.multiple_of(index * block, block), block)
 
-    def gather_copy(which, source, target, index, hop):
+    def gather_copy(which, target, index, hop):
         bit = side if hop == 0 else 1
         place = rows_of(index)
         return pltpu.make_async_remote_copy(
-            src_ref=source if source is not None else target.at[place],
+            src_ref=target.at[place],
             dst_ref=target.at[place],
             send_sem=gather_send.at[which, hop],
             recv_sem=gather_recv.at[which, hop],
@@ -106,46 +120,60 @@
             device_id_type=MESH,
         )
 
-    gather_copy(0, upstream, up_all, row, 0).start()
-    gather_copy(0, upstream, up_all, row, 1).start()
-
-    def take_up(cols):
-        up_all[rows_of(row), cols] = upstream[:, cols]
+    def start_copy(which):
+        if which == 0:
+            return pltpu.make_async_copy(upstream, up_all.at[rows_of(row)], start_sem.at[0])
+        return pltpu.make_async_copy(stash_inputs, kept, start_sem.at[1])
+
+    def slope_copy(unit):
+        cols = pl.ds(pl.multiple_of(chunk_of(unit) * width, width), width)
+        slot = lax.rem(unit, 2)
+        return pltpu.make_async_copy(
+            stash_hidden.at[:, :, cols], slopes.at[slot], slope_sem.at[slot]
+        )
+
+    def clear(cols):
         acc[:, cols] = jnp.zeros((tokens, cols.size), F32)
 
     def first_copy(index, start):
         slot = lax.rem(index, 2)
 
-        @pl.when(index < chunks)
-        def _():
-            place = pl.ds(pl.multiple_of(index * width, width), width)
+        place = pl.ds(pl.multiple_of(chunk_of(index) * width, width), width)
+
+        @pl.when(backward(index))
+        def _():
             copy = pltpu.make_async_copy(w_out.at[place], first_out.at[slot], first_sem.at[slot])
             copy.start() if start else copy.wait()
 
-        @pl.when(index >= chunks)
-        def _():
-            place = pl.ds(pl.multiple_of((index - chunks) * width, width), width)
+        @pl.when(jnp.logical_not(backward(index)))
+        def _():
             copy = pltpu.make_async_copy(w_in.at[:, place], first_in.at[slot], first_sem.at[slot])
             copy.start() if start else copy.wait()
 
     def second_copy(index, start):
         slot = lax.rem(index, 2)
 
-        @pl.when(index < chunks)
-        def _():
-            place = pl.ds(pl.multiple_of(index * width, width), width)
+        place = pl.ds(pl.multiple_of(chunk_of(index) * width, width), width)
+
+        @pl.when(backward(index))
+        def _():
             copy = pltpu.make_async_copy(w_in.at[:, place], second_in.at[slot], second_sem.at[slot])
             copy.start() if start else copy.wait()
 
-        @pl.when(index >= chunks)
-        def _():
-            place = pl.ds(pl.multiple_of((index - chunks) * width, width), width)
+        @pl.when(jnp.logical_not(backward(index)))
+        def _():
             copy = pltpu.make_async_copy(w_out.at[place], second_out.at[slot], second_sem.at[slot])
             copy.start() if start else copy.wait()
 
+    start_copy(0).start()
     first_copy(jnp.int32(0), True)
+    start_copy(1).start()
+    slope_copy(jnp.int32(0)).start()
+    first_copy(jnp.int32(1), True)
     second_copy(jnp.int32(0), True)
-    strips(features, strip, take_up)
+    start_copy(0).wait()
+    gather_copy(0, up_all, row, 0).start()
+    gather_copy(0, up_all, row, 1).start()
 
     lane = lax.broadcasted_iota(jnp.int32, (own_rows, LANE), 1)
 
@@ -183,48 +211,48 @@
         zero = jnp.zeros((own_rows, 1), F32)
         return lax.fori_loop(0, features // strip, one, (zero,) * 2)
 
-    def moments(ref):
+    def moments(read):
         def source(cols):
-            values = ref[:, cols].astype(F32)
+            values = read(cols)
             return values, values * values
 
         return reduced(source)
-
-    stat_sent[0] = packed(moments(fwd_in) + moments(bwd_in))
-    for away in range(1, n):
-        stat_copy(0, away).start()
-    sums = summed(0)
 
     def scale_of(total_sum, squares):
         mean = total_sum * inverse
         return mean, lax.rsqrt(squares * inverse - mean * mean + EPSILON)
 
-    stats[...] = packed(
-        scale_of(sums[:, 0:1], sums[:, 1:2]) + scale_of(sums[:, 2:3], sums[:, 3:4])
-    )
-
     def normalize(cols):
-        hat = (fwd_in[:, cols].astype(F32) - stats[:, 0:1]) * stats[:, 1:2]
+        hat = (fwd_in(cols) - stats[:, 0:1]) * stats[:, 1:2]
         normed_all[rows_of(row), cols] = (hat * gain[:, cols]).astype(BF16)
 
-    strips(features, strip, normalize)
-    gather_copy(1, None, normed_all, row, 0).start()
-    gather_copy(1, None, normed_all, row, 1).start()
+    def forward_sums():
+        start_copy(1).wait()
+        stat_sent[0] = packed(moments(fwd_in) + moments(bwd_in))
+        for away in range(1, n):
+            stat_copy(0, away).start()
+
+    def forward_norm():
+        sums = summed(0)
+        stats[...] = packed(
+            scale_of(sums[:, 0:1], sums[:, 1:2]) + scale_of(sums[:, 2:3], sums[:, 3:4])
+        )
+        strips(features, strip, normalize)
+        gather_copy(1, normed_all, row, 0).start()
+        gather_copy(1, normed_all, row, 1).start()
 
     def pass_on(which, target):
         far = flipped(row, side)
-        gather_copy(which, None, target, far, 0).wait_recv()
-        gather_copy(which, None, target, far, 2).start()
-
-    def gathered(which, target):
-        near = flipped(row, 1)
-        gather_copy(which, None, target, near, 1).wait_recv()
-        gather_copy(which, None, target, flipped(near, side), 2).wait_recv()
+        gather_copy(which, target, far, 0).wait_recv()
+        gather_copy(which, target, far, 2).start()
+
+    def gathered_near(which, target):
+        gather_copy(which, target, flipped(row, 1), 1).wait_recv()
+
+    def gathered_far(which, target):
+        gather_copy(which, target, flipped(flipped(row, 1), side), 2).wait_recv()
         for hop in range(3):
-            gather_copy(which, None, target, row, hop).wait_send()
-
-    pass_on(0, up_all)
-    gathered(0, up_all)
+            gather_copy(which, target, row, hop).wait_send()
 
     def neighbour(way):
         return jnp.minimum(col + 1, last) if way == 0 else jnp.maximum(col - 1, 0)
@@ -263,16 +291,23 @@
     def spread_origin(way, hop):
         return col - hop if way == 0 else col + hop
 
+    def sum_here(way, index, hop):
+        at = place_in_line(way)
+        return valid(index) & (at <= hop) & (at < last)
+
+    def spread_here(way, index, hop):
+        at = place_in_line(way)
+        return valid(index) & (at >= hop)
+
     def sum_step(index, hop):
         for way in range(2):
-            at = place_in_line(way)
-
-            @pl.when(valid(index) & (at <= hop) & (at < last))
+
+            @pl.when(sum_here(way, index, hop))
             def _():
                 target = sum_target(way, hop)
                 if hop > 0:
 
-                    @pl.when(at > 0)
+                    @pl.when(place_in_line(way) > 0)
                     def _():
                         sum_copy(way, index, hop - 1, target).wait_recv()
                         slot = lax.rem(index, n)
@@ -284,40 +319,38 @@
 
     def sum_sent(index, hop):
         for way in range(2):
-            at = place_in_line(way)
-
-            @pl.when(valid(index) & (at <= hop) & (at < last))
+
+            @pl.when(sum_here(way, index, hop))
             def _():
                 sum_copy(way, index, hop, sum_target(way, hop)).wait_send()
 
     def spread_step(index, hop):
         for way in range(2):
-            at = place_in_line(way)
-
-            @pl.when(valid(index) & (at >= hop))
+
+            @pl.when(spread_here(way, index, hop))
             def _():
                 origin = spread_origin(way, hop)
                 if hop > 0:
                     spread_copy(way, index, hop - 1, origin).wait_recv()
 
-                @pl.when(at < last)
+                @pl.when(place_in_line(way) < last)
                 def _():
                     spread_copy(way, index, hop, origin).start()
 
     def spread_sent(index, hop):
         for way in range(2):
-            at = place_in_line(way)
-
-            @pl.when(valid(index) & (at >= hop) & (at < last))
+
+            @pl.when(spread_here(way, index, hop) & (place_in_line(way) < last))
             def _():
                 spread_copy(way, index, hop, spread_origin(way, hop)).wait_send()
 
     def spread_done(index):
         for way in range(2):
+            origin = spread_origin(way, last)
 
             @pl.when(place_in_line(way) == last)
             def _():
-                spread_copy(way, index, n - 2, spread_origin(way, last)).wait_recv()
+                spread_copy(way, index, n - 2, origin).wait_recv()
 
     def activate(index):
         slot = lax.rem(index, n)
@@ -335,21 +368,27 @@
             def _():
                 total[...] += moved[way, lax.rem(index, 3), n - 2].astype(F32)
 
-        tile = min(STRIP, width)
-
-        @pl.when(index < chunks)
+        tile = STRIP if width % STRIP == 0 else LANE
+
+        @pl.when(backward(index))
         def _():
             for at in range(0, width, tile):
-                cols = pl.ds(pl.multiple_of(index * width + at, tile), tile)
-                slope = gelu_slope(bwd_hidden[:, cols].astype(F32))
+                slot_of = lax.rem(index, 2)
+                before = slopes[slot_of, 0, :, at : at + tile].astype(F32)
+                for other in range(1, slopes.shape[1]):
+                    before = jnp.where(
+                        bwd_slot == other,
+                        slopes[slot_of, other, :, at : at + tile].astype(F32),
+                        before,
+                    )
                 held[out_slot, block_of(col), at : at + tile] = (
-                    total[:, at : at + tile] * slope
+                    total[:, at : at + tile] * gelu_slope(before)
                 ).astype(BF16)
 
-        @pl.when(index >= chunks)
+        @pl.when(jnp.logical_not(backward(index)))
         def _():
             for at in range(0, width, tile):
-                cols = pl.ds(pl.multiple_of((index - chunks) * width + at, tile), tile)
+                cols = pl.ds(pl.multiple_of(chunk_of(index) * width + at, tile), tile)
                 values = total[:, at : at + tile] + b_in[:, cols]
                 saved[:, cols] = values.astype(BF16)
                 held[out_slot, block_of(col), at : at + tile] = gelu_value(values).astype(BF16)
@@ -360,9 +399,9 @@
     def first_product(index):
         slot = lax.rem(index, 2)
         out_slot = lax.rem(index, n)
-        tile = min(256, width)
-
-        @pl.when(index < chunks)
+        tile = 256 if width % 256 == 0 else width
+
+        @pl.when(backward(index))
         def _():
             for at in range(0, width, tile):
                 part[out_slot, :, at : at + tile] = lax.dot_general(
@@ -370,7 +409,7 @@
                     preferred_element_type=F32,
                 ).astype(BF16)
 
-        @pl.when(index >= chunks)
+        @pl.when(jnp.logical_not(backward(index)))
         def _():
             for at in range(0, width, tile):
                 part[out_slot, :, at : at + tile] = lax.dot_general(
@@ -384,7 +423,7 @@
         tile = min(256, features)
         group = 2 if features % (2 * tile) == 0 else 1
 
-        @pl.when(index < chunks)
+        @pl.when(backward(index))
         def _():
             @pl.loop(0, features // (tile * group))
             def _(step):
@@ -395,7 +434,7 @@
                         preferred_element_type=F32,
                     )
 
-        @pl.when(index >= chunks)
+        @pl.when(jnp.logical_not(backward(index)))
         def _():
             @pl.loop(0, features // (tile * group))
             def _(step):
@@ -406,12 +445,12 @@
                         preferred_element_type=F32,
                     )
 
-    def half_copy(which, k):
+    def half_copy(which, k, p):
         return pltpu.make_async_remote_copy(
-            src_ref=half_sent.at[k],
-            dst_ref=half_got.at[k],
-            send_sem=half_send.at[which, k],
-            recv_sem=half_recv.at[which, k],
+            src_ref=half_sent.at[k, p],
+            dst_ref=half_got.at[k, p],
+            send_sem=half_send.at[which, k, p],
+            recv_sem=half_recv.at[which, k, p],
             device_id={"row": flipped(row, 1)},
             device_id_type=MESH,
         )
@@ -444,44 +483,34 @@
             pl.semaphore_wait(half_free, 1)
         for k in (1, 0):
             index = flipped_by(row, 1 + side * k)
-
-            def cut(cols):
-                half_sent[k, :, cols] = acc[rows_of(index), cols].astype(BF16)
-
-            strips(features, strip, cut)
-            half_copy(which, k).start()
+            for p in range(pieces):
+                cols = pl.ds(p * piece, piece)
+                half_sent[k, p] = acc[rows_of(index), cols].astype(BF16)
+                half_copy(which, k, p).start()
 
     def fold_far(which):
-        half_copy(which, 1).wait_recv()
         if which == 1:
             pl.semaphore_wait(side_free, 1)
         far = flipped(row, side)
         for p in range(pieces):
+            half_copy(which, 1, p).wait_recv()
             cols = pl.ds(p * piece, piece)
-            side_sent[p] = (
-                acc[rows_of(far), cols] + half_got[1, :, cols].astype(F32)
-            ).astype(BF16)
+            side_sent[p] = (acc[rows_of(far), cols] + half_got[1, p].astype(F32)).astype(BF16)
             side_copy(which, p).start()
-        half_copy(which, 0).wait_recv()
-
-        def keep(cols):
-            own[:, cols] = acc[rows_of(row), cols] + half_got[0, :, cols].astype(F32)
-
-        strips(features, strip, keep)
+
+    def backward_own():
+        for p in range(pieces):
+            half_copy(0, 0, p).wait_recv()
+            cols = pl.ds(p * piece, piece)
+            own[:, cols] = acc[rows_of(row), cols] + half_got[0, p].astype(F32)
         for k in range(2):
-            half_copy(which, k).wait_send()
-        if which == 0:
-            pl.semaphore_signal(
-                half_free, 1, device_id={"row": flipped(row, 1)}, device_id_type=MESH
-            )
-
-            def clear(cols):
-                acc[:, cols] = jnp.zeros((tokens, cols.size), F32)
-
-            strips(features, strip, clear)
+            for p in range(pieces):
+                half_copy(0, k, p).wait_send()
+        pl.semaphore_signal(half_free, 1, device_id={"row": flipped(row, 1)}, device_id_type=MESH)
+        strips(features, strip, clear)
 
     def backward_hat(cols):
-        return (bwd_in[:, cols].astype(F32) - stats[:, 2:3]) * stats[:, 3:4]
+        return (bwd_in(cols) - stats[:, 2:3]) * stats[:, 3:4]
 
     def backward_sums():
         for p in range(pieces):
@@ -509,7 +538,7 @@
         def finish(cols):
             values = own[:, cols] - stats[:, 4:5] - backward_hat(cols) * stats[:, 5:6]
             final[0, :, cols] = (
-                upstream[:, cols].astype(F32) + stats[:, 3:4] * values
+                up_all[rows_of(row), cols].astype(F32) + stats[:, 3:4] * values
             ).astype(BF16)
 
         strips(features, strip, finish)
@@ -520,9 +549,15 @@
     steps = queue + turn
     middle = chunks - 1 + turn
 
+    def at_step(m, step, *actions):
+        @pl.when(m == step)
+        def _():
+            for action in actions:
+                action()
+
     def step(m, carry):
-        first_ready = valid(m)
         second = m - turn
+        ready = m - last
 
         for way in range(2):
 
@@ -530,50 +565,40 @@
             def _():
                 pl.semaphore_wait(credit.at[way], 1)
 
-        @pl.when(m + 1 < queue)
-        def _():
-            first_copy(m + 1, True)
-
-        @pl.when((second + 1 >= 1) & (second + 1 < queue))
+        @pl.when(m + 2 < queue)
+        def _():
+            first_copy(m + 2, True)
+
+        @pl.when((second >= 0) & (second + 1 < queue))
         def _():
             second_copy(second + 1, True)
 
-        for hop in range(1, n - 1):
+        @pl.when((ready >= 0) & (ready + 1 < chunks))
+        def _():
+            slope_copy(ready + 1).start()
+
+        for hop in range(n - 1):
             sum_step(m - hop, hop)
 
-        @pl.when(valid(m - last))
-        def _():
-            activate(m - last)
+        @pl.when((ready >= 0) & (ready < chunks))
+        def _():
+            slope_copy(ready).wait()
+
+        @pl.when(valid(ready))
+        def _():
+            activate(ready)
 
         for hop in range(n - 1):
-            spread_step(m - last - hop, hop)
-
-        @pl.when(m == min(4, chunks - 1))
-        def _():
-            pass_on(1, normed_all)
-
-        @pl.when(m == chunks)
-        def _():
-            gathered(1, normed_all)
-
-        @pl.when(first_ready)
-        def _():
-            first_copy(m, False)
-            first_product(m)
-
-        sum_step(m, 0)
-
-        @pl.when(m == middle + 1)
-        def _():
-            fold_far(0)
-
-        @pl.when(m == middle + 3)
-        def _():
-            backward_sums()
-
-        @pl.when(m == middle + 4)
-        def _():
-            backward_end()
+            spread_step(ready - hop, hop)
+
+        at_step(m, 6, lambda: pass_on(1, normed_all))
+        at_step(
+            m, chunks - 1,
+            lambda: gathered_near(1, normed_all), lambda: gathered_far(1, normed_all),
+        )
+        at_step(m, middle + 1, lambda: fold_far(0), backward_own)
+        at_step(m, middle + 3, backward_sums)
+        at_step(m, middle + 4, backward_end)
 
         @pl.when(valid(second))
         def _():
@@ -581,14 +606,17 @@
             second_copy(second, False)
             second_product(second)
 
-        @pl.when(m == middle)
-        def _():
-            fold_near(0)
+        at_step(m, middle, lambda: fold_near(0))
 
         for hop in range(n - 1):
             sum_sent(m - 1 - hop, hop)
             spread_sent(m - 1 - last - hop, hop)
 
+        @pl.when(m + 1 < queue)
+        def _():
+            first_copy(m + 1, False)
+            first_product(m + 1)
+
         for way in range(2):
 
             @pl.when((m < steps - 2) & (place_in_line(way) > 0))
@@ -599,19 +627,33 @@
 
         return carry
 
+    forward_sums()
+    strips(features, strip, clear)
+    forward_norm()
+    gathered_near(0, up_all)
+    pass_on(0, up_all)
+    gathered_far(0, up_all)
+    first_copy(jnp.int32(0), False)
+    first_product(jnp.int32(0))
     lax.fori_loop(0, steps, step, 0)
 
     fold_near(1)
     fold_far(1)
     for p in range(pieces):
+        half_copy(1, 0, p).wait_recv()
         cols = pl.ds(p * piece, piece)
+        own[:, cols] = acc[rows_of(row), cols] + (
+            half_got[0, p].astype(F32) + b_out[:, cols] + fwd_in(cols)
+        )
+    for p in range(pieces):
         side_copy(1, p).wait_recv()
-        final[1, :, cols] = (
-            own[:, cols] + side_got[p].astype(F32) + b_out[:, cols] + fwd_in[:, cols].astype(F32)
-        ).astype(BF16)
+        cols = pl.ds(p * piece, piece)
+        final[1, :, cols] = (own[:, cols] + side_got[p].astype(F32)).astype(BF16)
         final_copy(1, p).start()
     for p in range(pieces):
         side_copy(1, p).wait_send()
+        for k in range(2):
+            half_copy(1, k, p).wait_send()
     for which in range(2):
         for away in range(1, n):
             stat_copy(which, away).wait_send()
@@ -620,17 +662,18 @@
 
 
 def cut_count(features):
-    return max(p for p in range(1, 5) if features % (p * LANE) == 0)
+    return max(p for p in range(1, 9) if features % (p * LANE) == 0)
 
 
 def whole_layer(shape, *operands):
     n, ranks, sections = shape["col"], shape["row"], shape["section"]
-    fwd_in, w_in = operands[0], operands[7]
-    own_rows, features = fwd_in.shape
+    upstream, w_in = operands[6], operands[7]
+    own_rows, features = upstream.shape
+    depth = operands[4].shape[0]
     hidden_units = w_in.shape[1]
     tokens = own_rows * ranks
     block = tokens // n
-    width = WIDTH if n <= 8 else WIDTH // 2
+    width = WIDTH if n <= 8 else 256
     pieces = cut_count(features)
     dma = pltpu.SemaphoreType.DMA
     in_vmem = pl.BlockSpec(memory_space=pltpu.VMEM)
@@ -651,11 +694,15 @@
         pltpu.VMEM((own_rows, LANE), F32),
         pltpu.VMEM((2, own_rows, LANE), F32),
         pltpu.VMEM((2, n - 1, own_rows, LANE), F32),
-        pltpu.VMEM((2, own_rows, features), BF16),
-        pltpu.VMEM((2, own_rows, features), BF16),
+        pltpu.VMEM((2, pieces, own_rows, features // pieces), BF16),
+        pltpu.VMEM((2, pieces, own_rows, features // pieces), BF16),
         pltpu.VMEM((pieces, own_rows, features // pieces), BF16),
         pltpu.VMEM((pieces, own_rows, features // pieces), BF16),
         pltpu.VMEM((2, own_rows, features), BF16),
+        pltpu.VMEM((depth, own_rows, features), BF16),
+        pltpu.VMEM((2, depth, block, width), BF16),
+        dma((2,)),
+        dma((2,)),
         dma((2,)),
         dma((2,)),
         dma((2, 2, n - 1)),
@@ -666,8 +713,8 @@
         dma((2, 3)),
         dma((2, n - 1)),
         dma((2, n - 1)),
-        dma((2, 2)),
-        dma((2, 2)),
+        dma((2, 2, pieces)),
+        dma((2, 2, pieces)),
         dma((2, pieces)),
         dma((2, pieces)),
         dma((2, pieces)),
@@ -683,7 +730,7 @@
             jax.ShapeDtypeStruct((own_rows, features), BF16),
             jax.ShapeDtypeStruct((block, hidden_units), BF16),
         ),
-        in_specs=[in_vmem] * 7 + [anywhere] * 2,
+        in_specs=[pl.BlockSpec(memory_space=pltpu.SMEM)] + [in_vmem] * 3 + [anywhere] * 5,
         out_specs=(anywhere, anywhere, in_vmem),
         scratch_shapes=scratch,
         name="layer",
@@ -699,22 +746,8 @@
 
 
 def body(shape, stash_inputs, stash_hidden, grad_in, w_in, b_in, w_out, b_out, ln_gain, plan):
-    def picked(stash, slot):
-        return lax.dynamic_index_in_dim(stash[0], slot, 0, keepdims=False)
-
-    bwd_slot = plan[0, 0]
-    fwd_slot = plan[0, 1]
     act, grad, saved = whole_layer(
-        shape,
-        picked(stash_inputs, fwd_slot),
-        picked(stash_inputs, bwd_slot),
-        picked(stash_hidden, bwd_slot),
-        grad_in[0],
-        b_in,
-        b_out,
-        ln_gain,
-        w_in[0],
-        w_out[0],
+        shape, plan, b_in, b_out, ln_gain, stash_inputs[0], stash_hidden[0], grad_in[0], w_in[0], w_out[0]
     )
     return (act[None], grad[None], saved[None])
 

time: 381 us -> 365 us (0.958)
  Pallas kernels: 364 us -> 357 us
  local copies, waits for them, and re-layouts: 12 us -> 6.81 us
  between operations: 4.53 us -> 0.64 us
    pallas_call x1, Pallas kernels: 364 us -> 357 us  [whole_layer(): pl.pallas_call(functools.partial(kernel, n, ranks, sections, width, piece...]
    squeeze x2 -> x0, local copies, waits for them, and re-layouts: 5.3 us -> none  [picked(): return lax.dynamic_index_in_dim(stash[0], slot, 0, keepdims=False)]
where the time goes in v1:
time: 365 us
  Pallas kernels  357 us (98%)
  local copies, waits for them, and re-layouts  6.81 us (2%)
    pallas_call x1, Pallas kernels, whole_layer(): pl.pallas_call(functools.partial(kernel, n, ranks, sections, width, piece...  357 us

profile of v1, /device:TPU:0, one launch (start us, length us, event | category | flops | bytes accessed | tf_op | source)
XLA Modules:
  0.0 364.5 jit_solution(18316595375643534886)
XLA Ops:
  0.6 357.1 %layer.1 = (bf16[128,3072]{1,0:T(8,128)(2,1)}, bf16[128,3072]{1,0:T(8,128)(2,1)}, bf16[128,6144]{1,0:T(8,128)(2,1)}) custom-call(s32[1,2]{1,0:T(1,128)} %plan.1, f32[1,6144]{1,0:T(1,128)} %b_in.1, f32[1,3072]{1,0:T(1,128)} %b_out.1, f32[1,3072]{1,0:T(1,128)} %gain.1, bf16[4,128,3072]{2,1,0:T(8,128)(2,1)} %bitcast.14, bf16[4,128,6144]{2,1,0:T(8,128)(2,1)} %bitcast.13, ...), custom_call_target="tpu_custom_call" | custom-call | flops 77309411328 | bytes 150994944 | tf_op jit(solution)/shard_map/layer/pallas_call | solution.py:726
  357.7 2.1 copy.15
  359.8 2.1 copy.16
  361.8 2.7 copy.17
